TPU v7x, 32 devices: a whole 2x2x4 slice. The times are simulated.
32 devices in a mesh: vert: 8 (over z, y), col: 4 (over x, core).
Axes of the slice: x: 2, y: 2, z: 4, core: 2. Of those that a mesh axis runs over, the one named last changes fastest.
Arguments:
- coeffs: bfloat16 [64, 400], P(('vert', 'col')), may hold values from -6 to 6
- shape_basis: bfloat16 [400, 3, 656], P('col', None, 'vert'), may hold values from -0.3125 to 0.3125
- template: float32 [3, 656], P(None, 'vert'), may hold values from -6 to 6
- regressor: float32 [55, 656], P(None, 'vert'), may hold values from -0.5 to 0.5
- quaternions: float32 [64, 4, 55], P(('vert', 'col')), may hold values from -1.5 to 1.5, as said below
- translation: float32 [64, 3], P(('vert', 'col')), may hold values from -6 to 6
- parents: int32 [55], replicated, may hold values from 0 to 53, as said below
- skin_index: int32 [656, 4], P('vert'), may hold values from 0 to 54, all different within a row
- skin_raw: float32 [656, 4], P('vert'), may hold values from 0.1 to 1
Outputs:
- posed_vertices: bfloat16 [64, 3, 656], P(('vert', 'col'))
Inputs may be any that keep to these rules, and one draw needn't show every extreme that they name: parents[0] = 0 and parents[j] < j for j >= 1. `skin_index`: the four joints of a vertex differ. `quaternions`: component 0 lies in [0.5, 1.5].
All inputs are finite; a program needn't handle non-finite values.
Results may differ from a plain program's by a relative error of at most 0.0024.
Values may be sent and summed in bfloat16 or wider, within the bound.
A program may use at most 64 MiB of HBM per device.

v0:
```python
import functools

import jax
import jax.numpy as jnp
from jax import lax
from jax.experimental import pallas as pl
from jax.experimental.pallas import tpu as pltpu
from jax.sharding import PartitionSpec as P

MESH = pl.DeviceIdType.MESH
LANES = 128
HALF = 64
SUB = 8
F32 = jnp.float32
BF16 = jnp.bfloat16
EXACT = lax.Precision.HIGHEST


def iota(shape, dim):
    return lax.broadcasted_iota(jnp.int32, shape, dim)


def dot(a, b, precision=None):
    return jnp.dot(a, b, precision=precision, preferred_element_type=F32)


def dot_nt(a, b, precision=None):
    return lax.dot_general(a, b, (((1,), (1,)), ((), ())), precision=precision, preferred_element_type=F32)


def each(count, step):
    if count <= 16:
        for k in range(1, count):
            step(k)
    else:

        def one(k, carry):
            step(k)
            return carry

        lax.fori_loop(1, count, one, 0)


def kernel(
    n_vert,
    n_col,
    parents_hbm,
    coeffs_hbm,
    basis_hbm,
    template_hbm,
    regressor_hbm,
    quat_hbm,
    shift_hbm,
    index_hbm,
    raw_hbm,
    out_ref,
    parents,
    coeff_in,
    bas,
    template,
    regressor,
    quat,
    shift,
    index_in,
    raw_in,
    quat_rows,
    coeff_rows,
    blocks,
    sent,
    got,
    tree,
    state,
    diff,
    locals_ref,
    weights,
    local_s,
    coeff_s,
    coeff_r,
    bas_s,
    bas_r,
    index_s,
    index_r,
    raw_s,
    raw_r,
    sent_s,
    sent_r,
):
    me = lax.axis_index("vert")
    col = lax.axis_index("col")
    own, _ = coeffs_hbm.shape
    _, block, comps = basis_hbm.shape
    joints = regressor_hbm.shape[0]
    rows = n_vert * SUB

    barrier = pltpu.get_barrier_semaphore()

    def vert_peer(k):
        return (lax.rem(me + k, n_vert), col)

    def col_peer(k):
        return (me, lax.rem(col + k, n_col))

    each(n_vert, lambda k: pl.semaphore_signal(barrier, inc=1, device_id=vert_peer(k), device_id_type=MESH))
    each(n_col, lambda k: pl.semaphore_signal(barrier, inc=1, device_id=col_peer(k), device_id_type=MESH))

    pairs = [
        (coeffs_hbm, coeff_in.at[me]),
        (basis_hbm, bas.at[col]),
        (index_hbm, index_in.at[me]),
        (raw_hbm, raw_in.at[me]),
        (parents_hbm, parents),
        (quat_hbm, quat),
        (shift_hbm, shift),
        (template_hbm, template),
        (regressor_hbm, regressor),
    ]
    loads = [pltpu.make_async_copy(src, dst, local_s.at[i]) for i, (src, dst) in enumerate(pairs)]
    for load in loads:
        load.start()

    sub8 = iota((SUB, LANES), 0)
    lane8 = iota((SUB, LANES), 1)
    axis_lane = jnp.minimum((lane8 % SUB) // own, 2)
    quat_rows[...] = jnp.zeros(quat_rows.shape, F32)
    weights[...] = jnp.zeros(weights.shape, F32)
    tree[...] = jnp.zeros(tree.shape, F32)
    state[...] = jnp.zeros(state.shape, F32)
    diff[...] = jnp.zeros(diff.shape, F32)
    sent[...] = jnp.zeros(sent.shape, F32)
    for load in loads:
        load.wait()

    def copies(src, dst, send, recv, peer_of):
        def make(k):
            return pltpu.make_async_remote_copy(
                src_ref=src, dst_ref=dst, send_sem=send.at[k], recv_sem=recv.at[k], device_id=peer_of(k), device_id_type=MESH
            )

        return make

    coeff_copy = copies(coeff_in.at[me], coeff_in.at[me], coeff_s, coeff_r, vert_peer)
    bas_copy = copies(bas.at[col], bas.at[col], bas_s, bas_r, col_peer)
    index_copy = copies(index_in.at[me], index_in.at[me], index_s, index_r, vert_peer)
    raw_copy = copies(raw_in.at[me], raw_in.at[me], raw_s, raw_r, vert_peer)

    pl.semaphore_wait(barrier, n_vert + n_col - 2)
    each(n_col, lambda k: bas_copy(k).start())
    lower = 1 - me // (n_vert // 2)
    each(n_vert, lambda k: coeff_copy(k + lower * (n_vert - 2 * k)).start())
    each(n_vert, lambda k: index_copy(k).start())
    each(n_vert, lambda k: raw_copy(k).start())

    for c in range(own):
        quat_rows[4 * c : 4 * c + 4, 0:joints] = quat[c]
    q_row = iota((LANES, SUB), 0)
    q_col = iota((LANES, SUB), 1)
    w, x, y, z = [
        jnp.transpose(dot((q_col == (q_row % own) * 4 + comp).astype(F32), quat_rows[...], EXACT))[0:HALF] for comp in range(4)
    ]
    s = 2.0 / (w * w + x * x + y * y + z * z)
    matrix = [
        [1.0 - s * (y * y + z * z), s * (x * y - w * z), s * (x * z + w * y)],
        [s * (x * y + w * z), 1.0 - s * (x * x + z * z), s * (y * z - w * x)],
        [s * (x * z - w * y), s * (y * z + w * x), 1.0 - s * (x * x + y * y)],
    ]
    for m in range(3):
        for b in range(3):
            locals_ref[m, pl.ds(b, HALF, stride=SUB), :] = matrix[m][b]

    def compose(j, above):
        at = pl.multiple_of(j * SUB, SUB)
        new = jnp.zeros((SUB, LANES), F32)
        for m in range(3):
            new = new + jnp.broadcast_to(above[m : m + 1, :], (SUB, LANES)) * locals_ref[m, pl.ds(at, SUB), :]
        mine = above + (lane8 % HALF == j).astype(F32)
        new = jnp.where(sub8 < 3, new, jnp.where(sub8 == 3, mine, 0.0))
        if isinstance(j, int):
            new = new + jnp.where((sub8 == 3) & (lane8 == joints), 1.0, 0.0)
        tree[j] = new
        state[pl.ds(at, SUB), :] = new
        diff[pl.ds(at, SUB), :] = above - new

    def descend(j, carry):
        compose(j, tree[parents[j]])
        return carry

    compose(0, (axis_lane == sub8).astype(F32))
    lax.fori_loop(1, joints, descend, 0)

    def flipped(ref, m, n):
        value = ref[pl.ds(m, HALF, stride=SUB), :]
        return jnp.transpose(jnp.concatenate([value, value], axis=0))[0:n]

    gains = [flipped(diff, m, SUB) for m in range(3)]
    gains = [jnp.where(lane8 < HALF, gain, 0.0) for gain in gains]
    factors = jnp.concatenate(
        [flipped(state, m, SUB)[:, 0:HALF] for m in range(3)] + [flipped(state, 3, HALF)[:, 0:HALF]], axis=0
    )
    moves = jnp.concatenate([shift[...]] * (SUB // own), axis=0)
    m_axis = jnp.minimum(iota(moves.shape, 0) // own, 2)
    moves = jnp.sum(jnp.where(iota(moves.shape, 1) == m_axis, moves, 0.0), axis=1, keepdims=True)
    moves = jnp.where(lane8 == joints, moves, 0.0)

    each(n_vert, lambda k: coeff_copy(k).wait_recv())
    for i in range(n_vert):
        one = coeff_in[i].astype(F32)
        coeff_rows[i * SUB : (i + 1) * SUB, 0 : n_col * comps] = jnp.concatenate([one] * (SUB // own), axis=0)
    for kb in range(n_col):
        blocks[kb] = coeff_rows[:, kb * comps : (kb + 1) * comps].astype(BF16)

    totals = [template[m : m + 1, :] + dot_nt(blocks[col], bas[col, m]) for m in range(3)]
    for k in range(1, n_col):
        bas_copy(k).wait_recv()
        source = lax.rem(col + n_col - k, n_col)
        totals = [totals[m] + dot_nt(blocks[source], bas[source, m]) for m in range(3)]
    r_axis = jnp.minimum((iota((rows, block), 0) % SUB) // own, 2)
    full = jnp.where(r_axis == 0, totals[0], jnp.where(r_axis == 1, totals[1], totals[2]))
    share = dot_nt(full, regressor[...], EXACT)
    sent[:, 0, :, 0:block] = full.astype(BF16).astype(F32).reshape(n_vert, SUB, block)
    sent[:, 1, :, 0:joints] = share.reshape(n_vert, SUB, joints)

    def sent_copy(k):
        target = lax.rem(me + k, n_vert)
        return pltpu.make_async_remote_copy(
            src_ref=sent.at[target],
            dst_ref=got.at[me],
            send_sem=sent_s.at[k],
            recv_sem=sent_r.at[k],
            device_id=(target, col),
            device_id_type=MESH,
        )

    each(n_vert, lambda k: sent_copy(k + lower * (n_vert - 2 * k)).start())
    got[me] = sent[me]

    each(n_vert, lambda k: index_copy(k).wait_recv())
    each(n_vert, lambda k: raw_copy(k).wait_recv())
    joint_row = iota((HALF, block), 0)
    for i in range(n_vert):
        raw = raw_in[i]
        raw = raw / jnp.sum(raw, axis=0, keepdims=True)
        index = index_in[i]
        grid = jnp.zeros((HALF, block), F32)
        for slot in range(raw.shape[0]):
            grid = jnp.where(index[slot : slot + 1, :] == joint_row, raw[slot : slot + 1, :], grid)
        weights[:, i * LANES : i * LANES + block] = grid
    blended = dot(factors, weights[...], EXACT)
    turns = [blended[m * SUB : (m + 1) * SUB] for m in range(3)]
    upper = blended[3 * SUB :]
    upper_hi = upper.astype(BF16)
    upper_lo = (upper - upper_hi.astype(F32)).astype(BF16)
    upper_all = jnp.concatenate([upper_hi, upper_lo, upper_hi], axis=0)

    def rows_of(tile):
        spun = [tile] + [pltpu.roll(tile, own * q, 0) for q in range(1, SUB // own)]
        count = SUB // own
        result = []
        for m in range(3):
            value = spun[(-m) % count]
            for q in range(1, count):
                value = jnp.where(sub8 // own == q, spun[(q - m) % count], value)
            result.append(value)
        return result

    each(n_vert, lambda k: sent_copy(k).wait_recv())
    summed = got[0, 1]
    for i in range(1, n_vert):
        summed = summed + got[i, 1]
    places = rows_of(summed)
    term = moves
    for m in range(3):
        term = term + gains[m] * places[m]
    term_hi = term.astype(BF16)
    term_lo = (term - term_hi.astype(F32)).astype(BF16)
    term_all = jnp.concatenate([term_hi[:, 0:HALF], term_hi[:, 0:HALF], term_lo[:, 0:HALF]], axis=1)
    moved = dot(term_all, upper_all)

    n_cols = -(-n_vert * block // LANES) + 1
    columns = [None] * n_cols

    def put(q, value):
        columns[q] = value if columns[q] is None else columns[q] + value

    for i in range(n_vert):
        q, r = divmod(i * block, LANES)
        at = slice(i * LANES, (i + 1) * LANES)
        shaped = rows_of(got[i, 0])
        tile = moved[:, at]
        for m in range(3):
            tile = tile + turns[m][:, at] * shaped[m]
        if r:
            tile = pltpu.roll(tile, r, 1)
        if r + block > LANES:
            put(q, jnp.where(lane8 >= r, tile, 0.0))
            put(q + 1, jnp.where(lane8 < r, tile, 0.0))
        else:
            put(q, tile)
    width = n_vert * block
    for q in range(n_cols):
        size = min(LANES, width - q * LANES)
        if size > 0:
            value = columns[q].astype(out_ref.dtype)
            for a in range(3):
                out_ref[a, :, q * LANES : q * LANES + size] = value[own * a : own * (a + 1), 0:size]

    each(n_vert, lambda k: coeff_copy(k).wait_send())
    each(n_col, lambda k: bas_copy(k).wait_send())
    each(n_vert, lambda k: index_copy(k).wait_send())
    each(n_vert, lambda k: raw_copy(k).wait_send())
    each(n_vert, lambda k: sent_copy(k).wait_send())


def body(n_vert, n_col, coeffs, shape_basis, template, regressor, quaternions, translation, parents, skin_index, skin_raw):
    own, total = coeffs.shape
    comps, _, block = shape_basis.shape
    joints = regressor.shape[0]
    slots = skin_index.shape[1]
    vmem = pl.BlockSpec(memory_space=pltpu.VMEM)
    anywhere = pl.BlockSpec(memory_space=pl.ANY)
    dma = pltpu.SemaphoreType.DMA
    out = pl.pallas_call(
        functools.partial(kernel, n_vert, n_col),
        out_shape=jax.ShapeDtypeStruct((3, own, n_vert * block), BF16),
        in_specs=[anywhere] * 9,
        out_specs=vmem,
        scratch_shapes=[
            pltpu.SMEM((joints,), jnp.int32),
            pltpu.VMEM((n_vert, own, total), BF16),
            pltpu.VMEM((n_col, 3, block, comps), BF16),
            pltpu.VMEM((3, block), F32),
            pltpu.VMEM((joints, block), F32),
            pltpu.VMEM((own, 4, joints), F32),
            pltpu.VMEM((own, 3), F32),
            pltpu.VMEM((n_vert, slots, block), jnp.int32),
            pltpu.VMEM((n_vert, slots, block), F32),
            pltpu.VMEM((SUB, LANES), F32),
            pltpu.VMEM((n_vert * SUB, total), F32),
            pltpu.VMEM((n_col, n_vert * SUB, comps), BF16),
            pltpu.VMEM((n_vert, 2, SUB, LANES), F32),
            pltpu.VMEM((n_vert, 2, SUB, LANES), F32),
            pltpu.VMEM((joints, SUB, LANES), F32),
            pltpu.VMEM((HALF * SUB, LANES), F32),
            pltpu.VMEM((HALF * SUB, LANES), F32),
            pltpu.VMEM((3, HALF * SUB, LANES), F32),
            pltpu.VMEM((HALF, n_vert * LANES), F32),
            dma((9,)),
            dma((n_vert,)),
            dma((n_vert,)),
            dma((n_col,)),
            dma((n_col,)),
            dma((n_vert,)),
            dma((n_vert,)),
            dma((n_vert,)),
            dma((n_vert,)),
            dma((n_vert,)),
            dma((n_vert,)),
        ],
        compiler_params=pltpu.CompilerParams(collective_id=0, has_side_effects=True),
    )(
        parents,
        coeffs,
        jnp.transpose(shape_basis, (1, 2, 0)),
        template,
        regressor,
        quaternions,
        translation,
        jnp.transpose(skin_index),
        jnp.transpose(skin_raw),
    )
    return jnp.transpose(out, (1, 0, 2))


def solution(mesh):
    in_specs = (
        P(("vert", "col"), None),
        P("col", None, "vert"),
        P(None, "vert"),
        P(None, "vert"),
        P(("vert", "col"), None, None),
        P(("vert", "col"), None),
        P(),
        P("vert", None),
        P("vert", None),
    )
    out_specs = P(("vert", "col"), None, None)
    step = functools.partial(body, mesh.shape["vert"], mesh.shape["col"])
    return jax.shard_map(step, mesh=mesh, in_specs=in_specs, out_specs=out_specs, check_vma=False)
```

profile of v0, /device:TPU:0, one launch (start us, length us, event | category | flops | bytes accessed | tf_op | source)
XLA Modules:
  0.0 17.6 jit_solution(5564068067911720812)
XLA Ops:
  0.0 16.3 %shard_map.91 = bf16[3,2,656]{2,1,0:T(2,128)(2,1)} custom-call(s32[55]{0:T(128)} %parents_hbm.1, bf16[2,400]{1,0:T(2,128)(2,1)} %coeffs_hbm.1, bf16[3,82,100]{2,1,0:T(8,128)(2,1)} %bitcast.4, f32[3,82]{1,0:T(4,128)} %template_hbm.1, f32[55,82]{1,0:T(8,128)} %regressor_hbm.1, f32[2,4,55]{2,1,0:T(4,128)} %quat_hbm.1, f32[2,3]{1,0:T(2,128)} %shift_hbm.1, ...), custom_call_target="tpu_custom_call" | custom-call | tf_op jit(solution)/shard_map/pallas_call | solution.py:321
  16.3 1.3 %copy.11 = bf16[2,3,656]{2,0,1:T(2,128)(2,1)} copy(bf16[2,3,656]{2,0,1:T(2,128)(2,1)} %bitcast.5) | data formatting | bytes 15744
where the time goes:
time: 17.8 us; the launch traced here: 17.6 us
  Pallas kernels  16.3 us (92%)
  local copies, waits for them, and re-layouts  1.31 us (7%)
    pallas_call x1, Pallas kernels, body(): pl.pallas_call(functools.partial(kernel, n_vert, n_col), out_shape=jax.Sh...  16.3 us
    unnamed x1, local copies, waits for them, and re-layouts  1.31 us

commit v1 on v0

--- a/solution.py
+++ b/solution.py
@@ -320,7 +320,7 @@
     dma = pltpu.SemaphoreType.DMA
     out = pl.pallas_call(
         functools.partial(kernel, n_vert, n_col),
-        out_shape=jax.ShapeDtypeStruct((3, own, n_vert * block), BF16),
+        out_shape=pltpu.VMEM((3, own, n_vert * block), BF16),
         in_specs=[anywhere] * 9,
         out_specs=vmem,
         scratch_shapes=[

time: 17.8 us -> 16.5 us (0.927)
  local copies, waits for them, and re-layouts: 1.31 us -> 0.6 us
  Pallas kernels: 16.3 us -> 15.7 us
    unnamed x1, local copies, waits for them, and re-layouts: 1.31 us -> 0.6 us
    pallas_call x1, Pallas kernels: 16.3 us -> 15.7 us  [body(): pl.pallas_call(functools.partial(kernel, n_vert, n_col), out_shape=pltpu....]
where the time goes in v1:
time: 16.5 us; the launch traced here: 16.3 us
  Pallas kernels  15.7 us (95%)
  local copies, waits for them, and re-layouts  0.6 us (4%)
    pallas_call x1, Pallas kernels, body(): pl.pallas_call(functools.partial(kernel, n_vert, n_col), out_shape=pltpu....  15.7 us
    unnamed x1, local copies, waits for them, and re-layouts  0.6 us

profile of v1, /device:TPU:0, one launch (start us, length us, event | category | flops | bytes accessed | tf_op | source)
XLA Modules:
  0.0 16.3 jit_solution(17529898354201749403)
XLA Ops:
  0.0 15.7 %shard_map.91 = bf16[3,2,656]{2,1,0:T(2,128)(2,1)S(1)} custom-call(s32[55]{0:T(128)} %parents_hbm.1, bf16[2,400]{1,0:T(2,128)(2,1)} %coeffs_hbm.1, bf16[3,82,100]{2,1,0:T(8,128)(2,1)} %bitcast.5, f32[3,82]{1,0:T(4,128)} %template_hbm.1, f32[55,82]{1,0:T(8,128)} %regressor_hbm.1, f32[2,4,55]{2,1,0:T(4,128)} %quat_hbm.1, f32[2,3]{1,0:T(2,128)} %shift_hbm.1, ...), custom_call_target="tpu_custom_call" | custom-call | tf_op jit(solution)/shard_map/pallas_call | solution.py:321
  15.7 0.6 %copy.11 = bf16[2,3,656]{2,0,1:T(2,128)(2,1)} copy(bf16[2,3,656]{2,0,1:T(2,128)(2,1)S(1)} %bitcast.4) | data formatting | bytes 15744

commit v2 on v1

v2 whole, which is shorter than its diff:
```python
import functools

import jax
import jax.numpy as jnp
from jax import lax
from jax.experimental import pallas as pl
from jax.experimental.pallas import tpu as pltpu
from jax.sharding import PartitionSpec as P

MESH = pl.DeviceIdType.MESH
LANES = 128
HALF = 64
SUB = 8
PARTS = 3
F32 = jnp.float32
BF16 = jnp.bfloat16
EXACT = lax.Precision.HIGHEST


def iota(shape, dim):
    return lax.broadcasted_iota(jnp.int32, shape, dim)


def dot(a, b, precision=None):
    return jnp.dot(a, b, precision=precision, preferred_element_type=F32)


def dot_nt(a, b, precision=None):
    return lax.dot_general(a, b, (((1,), (1,)), ((), ())), precision=precision, preferred_element_type=F32)


def each(first, count, step):
    if count - first <= 16:
        for k in range(first, count):
            step(k)
    else:

        def one(k, carry):
            step(k)
            return carry

        lax.fori_loop(first, count, one, 0)


def split(value):
    parts = []
    for _ in range(PARTS):
        part = value.astype(BF16)
        value = value - part.astype(F32)
        parts.append(part)
    return parts


def kernel(
    n_vert,
    n_col,
    parents_hbm,
    coeffs_hbm,
    basis_hbm,
    template_hbm,
    regressor_hbm,
    quat_hbm,
    shift_hbm,
    index_hbm,
    raw_hbm,
    out_ref,
    parents,
    coeff_in,
    bas,
    template,
    regressor,
    quat,
    shift,
    index_in,
    raw_in,
    quat_rows,
    coeff_out,
    coeff_got,
    passed,
    coeff_rows,
    skin_out,
    skin_got,
    spread,
    wide,
    table,
    bias,
    product,
    lead,
    sent,
    got,
    tree,
    state,
    diff,
    locals_ref,
    weights,
    local_s,
    bas_s,
    bas_r,
    coeff_s,
    coeff_r,
    passed_s,
    passed_r,
    relay_s,
    skin_s,
    skin_r,
    sent_s,
    sent_r,
):
    me = lax.axis_index("vert")
    col = lax.axis_index("col")
    own, total = coeffs_hbm.shape
    _, block, comps = basis_hbm.shape
    joints = regressor_hbm.shape[0]
    slots = index_hbm.shape[0]
    groups = n_col // 2
    n_src = n_vert * groups
    room = LANES - block
    extra = joints - room

    group = col // 2
    side = col % 2
    mine = me * groups + group
    first = mine == 0
    hub = n_vert // 2
    is_hub = (me == hub) & (col == 1)
    partner = (me, 2 * group + 1 - side)
    upper = me // hub

    def place(i, parity):
        return (i // groups, 2 * (i % groups) + parity)

    def across(i):
        return place(i, 1 - side)

    def far_first(j):
        return j + (1 - upper) * (n_src - 1 - 2 * j)

    barrier = pltpu.get_barrier_semaphore()

    def hello(target):
        pl.semaphore_signal(barrier, inc=1, device_id=target, device_id_type=MESH)

    @pl.when(is_hub)
    def _():
        hello((0, 1))

    @pl.when(is_hub | first)
    def _():
        hello(across(0))

    @pl.when((side == 1) & jnp.logical_not(is_hub))
    def _():
        hello((hub, 1))

    each(1, n_src, lambda j: hello(across(n_src - j)))

    pairs = [
        (coeffs_hbm, coeff_in),
        (basis_hbm, bas.at[side]),
        (index_hbm, index_in),
        (raw_hbm, raw_in),
        (parents_hbm, parents),
        (quat_hbm, quat),
        (shift_hbm, shift),
        (template_hbm, template),
        (regressor_hbm, regressor),
    ]
    loads = [pltpu.make_async_copy(src, dst, local_s.at[i]) for i, (src, dst) in enumerate(pairs)]
    for load in loads:
        load.start()

    sub8 = iota((SUB, LANES), 0)
    lane8 = iota((SUB, LANES), 1)
    axis_lane = jnp.minimum((lane8 % SUB) // own, 2)
    quat_rows[...] = jnp.zeros(quat_rows.shape, F32)
    weights[...] = jnp.zeros(weights.shape, F32)
    tree[...] = jnp.zeros(tree.shape, F32)
    state[...] = jnp.zeros(state.shape, F32)
    diff[...] = jnp.zeros(diff.shape, F32)
    coeff_out[...] = jnp.zeros(coeff_out.shape, BF16)
    spread[...] = jnp.zeros(spread.shape, F32)
    wide[...] = jnp.zeros(wide.shape, F32)
    bias[...] = jnp.zeros(bias.shape, F32)
    for load in loads:
        load.wait()

    mine_coeffs = coeff_in[...].astype(F32)
    for kb in range(n_col):
        coeff_out[kb, :, 0:comps] = mine_coeffs[:, kb * comps : (kb + 1) * comps].astype(BF16)
    raw = raw_in[...]
    skin_out[0] = index_in[...].astype(F32)
    skin_out[1] = raw / jnp.sum(raw, axis=0, keepdims=True)

    def remote(src, dst, send, recv, target):
        return pltpu.make_async_remote_copy(
            src_ref=src, dst_ref=dst, send_sem=send, recv_sem=recv, device_id=target, device_id_type=MESH
        )

    bas_copy = remote(bas.at[side], bas.at[side], bas_s, bas_r, partner)

    def bas_arrival():
        remote(bas.at[1 - side], bas.at[1 - side], bas_s, bas_r, partner).wait_recv()

    def two(i):
        return pl.ds(2 * (i % groups), 2)

    def coeff_copy(i):
        return remote(coeff_out.at[two(i)], coeff_got.at[mine], coeff_s.at[i], coeff_r.at[mine], across(i))

    def coeff_arrival(i):
        remote(coeff_out.at[pl.ds(0, 2)], coeff_got.at[i], coeff_s.at[i], coeff_r.at[i], across(i)).wait_recv()

    pass_copy = remote(coeff_out, passed.at[side], passed_s, passed_r.at[side], (hub, 1))

    def pass_arrival(k):
        remote(coeff_out, passed.at[k], passed_s, passed_r.at[k], (0, k)).wait_recv()

    def relay_copy(k, i):
        return remote(passed.at[k, two(i)], coeff_got.at[0], relay_s.at[k, i], coeff_r.at[0], place(i, 1 - k))

    def skin_copy(i):
        return remote(skin_out, skin_got.at[me], skin_s.at[i], skin_r.at[me], across(i))

    def skin_arrival(v):
        remote(skin_out, skin_got.at[v], skin_s.at[0], skin_r.at[v], partner).wait_recv()

    def tile(ref, i):
        start = i * SUB if isinstance(i, int) else pl.multiple_of(i * SUB, SUB)
        return ref.at[pl.ds(start, SUB)]

    def sent_copy(i):
        return remote(tile(sent, i), tile(got, mine), sent_s.at[i], sent_r.at[mine], across(i))

    lead_copy = remote(lead, tile(got, mine), sent_s.at[0], sent_r.at[mine], across(0))

    def sent_arrival(i):
        remote(tile(sent, i), tile(got, i), sent_s.at[i], sent_r.at[i], across(i)).wait_recv()

    hub_index = hub * groups
    expected = n_src + is_hub.astype(jnp.int32) * (n_src - 1)
    pl.semaphore_wait(barrier, jnp.where(first, 2, expected))
    bas_copy.start()

    @pl.when(first)
    def _():
        pass_copy.start()

    @pl.when(jnp.logical_not(first))
    def _():
        each(0, n_src, lambda j: coeff_copy(far_first(j)).start())

    @pl.when(is_hub)
    def _():
        pass_arrival(0)
        each(hub_index + 1, n_src, lambda i: relay_copy(0, i).start())
        pltpu.make_async_copy(passed.at[0, two(hub_index)], coeff_got.at[0], coeff_r.at[0]).start()
        each(0, hub_index, lambda i: relay_copy(0, i).start())
        pass_arrival(1)
        each(0, n_src, lambda j: relay_copy(1, n_src - 1 - j).start())

    @pl.when(group == groups - 1)
    def _():
        each(0, n_src, lambda j: skin_copy(far_first(j)).start())

    for c in range(own):
        quat_rows[4 * c : 4 * c + 4, 0:joints] = quat[c]
    q_row = iota((LANES, SUB), 0)
    q_col = iota((LANES, SUB), 1)
    w, x, y, z = [
        jnp.transpose(dot((q_col == (q_row % own) * 4 + comp).astype(F32), quat_rows[...], EXACT))[0:HALF] for comp in range(4)
    ]
    s = 2.0 / (w * w + x * x + y * y + z * z)
    matrix = [
        [1.0 - s * (y * y + z * z), s * (x * y - w * z), s * (x * z + w * y)],
        [s * (x * y + w * z), 1.0 - s * (x * x + z * z), s * (y * z - w * x)],
        [s * (x * z - w * y), s * (y * z + w * x), 1.0 - s * (x * x + y * y)],
    ]
    for m in range(3):
        for b in range(3):
            locals_ref[m, pl.ds(b, HALF, stride=SUB), :] = matrix[m][b]

    def compose(j, above):
        at = pl.multiple_of(j * SUB, SUB)
        new = jnp.zeros((SUB, LANES), F32)
        for m in range(3):
            new = new + jnp.broadcast_to(above[m : m + 1, :], (SUB, LANES)) * locals_ref[m, pl.ds(at, SUB), :]
        mine = above + (lane8 % HALF == j).astype(F32)
        new = jnp.where(sub8 < 3, new, jnp.where(sub8 == 3, mine, 0.0))
        if isinstance(j, int):
            new = new + jnp.where((sub8 == 3) & (lane8 == joints), 1.0, 0.0)
        tree[j] = new
        state[pl.ds(at, SUB), :] = new
        diff[pl.ds(at, SUB), :] = above - new

    def descend(j, carry):
        compose(j, tree[parents[j]])
        return carry

    compose(0, (axis_lane == sub8).astype(F32))
    lax.fori_loop(1, joints, descend, 0)

    for m in range(3):
        spread[m, block:LANES, :] = regressor[0:room, :]
        spread[m, extra * m : extra * (m + 1), :] = regressor[room:joints, :]
    for m in range(3):
        base = dot_nt(template[...], spread[m], EXACT)[m : m + 1, :]
        spot = iota(base.shape, 1)
        bias[m : m + 1, :] = jnp.where(spot >= block, base, 0.0)
        bias[m : m + 1, 0:block] = template[m : m + 1, :]
        mark = (spot >= extra * m) & (spot < extra * (m + 1))
        bias[3:4, :] = bias[3:4, :] + jnp.where(mark, base, 0.0)
    spread_parts = [jnp.concatenate(split(spread[m]), axis=0) for m in range(3)]

    def lay(b, at):
        for m in range(3):
            one = bas[b, m]
            sums = dot(spread_parts[m], one)
            sums = sums[0:LANES] + sums[LANES : 2 * LANES] + sums[2 * LANES :]
            wide[m * LANES : m * LANES + block, at : at + comps] = one.astype(F32)
            wide[m * LANES + block : (m + 1) * LANES, at : at + comps] = sums[block:]
            row = 3 * LANES + extra * m
            wide[row : row + extra, at : at + comps] = sums[extra * m : extra * (m + 1)]

    bas_arrival()
    for b in range(2):
        lay(b, b * LANES)
    for p, part in enumerate(split(wide[...])):
        table[p] = part

    has_bias = (group == 0).astype(F32)

    def partial(rows, q):
        at = slice(q * LANES, (q + 1) * LANES)
        value = bias[q : q + 1, :] * has_bias
        for p in range(PARTS):
            value = value + dot_nt(rows, table[p, at, :])
        return value

    coeff_arrival(0)
    rows = jnp.concatenate([coeff_got[0, 0], coeff_got[0, 1]], axis=1)
    lead[...] = jnp.concatenate([partial(rows, q) for q in range(4)], axis=0)
    lead_copy.start()

    each(1, n_src, coeff_arrival)
    per = SUB // own

    def gather(step):
        for b in range(2):
            rows = [coeff_got[step * per + i, b].astype(F32) for i in range(per)]
            start = step * SUB if isinstance(step, int) else pl.multiple_of(step * SUB, SUB)
            coeff_rows[pl.ds(start, SUB), b * LANES : (b + 1) * LANES] = jnp.concatenate(rows, axis=0)

    each(0, n_src // per, gather)
    rows = coeff_rows[...].astype(BF16)
    for q in range(4):
        product[q] = partial(rows, q)
    for q in range(4):
        for c in range(own):
            value = product[q, pl.ds(c, n_src, stride=own), :]
            sent[pl.ds(q * own + c, n_src, stride=SUB), :] = value
    each(0, n_src - 1, lambda j: sent_copy(1 + j + (1 - upper) * (n_src - 2 - 2 * j)).start())

    def flipped(ref, m, n):
        value = ref[pl.ds(m, HALF, stride=SUB), :]
        return jnp.transpose(jnp.concatenate([value, value], axis=0))[0:n]

    gains = [flipped(diff, m, SUB) for m in range(3)]
    gains = [jnp.where(lane8 < HALF, gain, 0.0) for gain in gains]
    factors = jnp.concatenate(
        [flipped(state, m, SUB)[:, 0:HALF] for m in range(3)] + [flipped(state, 3, HALF)[:, 0:HALF]], axis=0
    )
    moves = jnp.concatenate([shift[...]] * (SUB // own), axis=0)
    m_axis = jnp.minimum(iota(moves.shape, 0) // own, 2)
    moves = jnp.sum(jnp.where(iota(moves.shape, 1) == m_axis, moves, 0.0), axis=1, keepdims=True)
    moves = jnp.where(lane8 == joints, moves, 0.0)

    each(0, n_vert, skin_arrival)
    joint_row = iota((HALF, block), 0).astype(F32)
    for i in range(n_vert):
        grid = jnp.zeros((HALF, block), F32)
        for slot in range(slots):
            grid = jnp.where(skin_got[i, 0, slot : slot + 1, :] == joint_row, skin_got[i, 1, slot : slot + 1, :], grid)
        weights[:, i * LANES : i * LANES + block] = grid
    blended = dot(factors, weights[...], EXACT)
    turns = [blended[m * SUB : (m + 1) * SUB] for m in range(3)]
    above_hi = blended[3 * SUB :].astype(BF16)
    above_lo = (blended[3 * SUB :] - above_hi.astype(F32)).astype(BF16)
    above_all = jnp.concatenate([above_hi, above_lo, above_hi], axis=0)

    def rows_of(value):
        count = SUB // own
        spun = [value] + [pltpu.roll(value, own * q, 0) for q in range(1, count)]
        result = []
        for m in range(3):
            one = spun[(-m) % count]
            for q in range(1, count):
                one = jnp.where(sub8 // own == q, spun[(q - m) % count], one)
            result.append(one)
        return result

    each(0, n_src, sent_arrival)
    tiles = []
    for i in range(n_vert):
        at = i * groups * SUB
        value = got[at : at + SUB, :]
        for q in range(1, groups):
            value = value + got[at + q * SUB : at + (q + 1) * SUB, :]
        tiles.append(value)
    summed = tiles[0]
    for value in tiles[1:]:
        summed = summed + value
    spots = jnp.where(lane8 < room, pltpu.roll(summed, room, 1), 0.0)
    for m in range(3):
        moved = pltpu.roll(pltpu.roll(summed, (room - extra * m) % LANES, 1), (own * (m - 3)) % SUB, 0)
        spots = jnp.where((sub8 // own == m) & (lane8 >= room) & (lane8 < joints), moved, spots)
    places = rows_of(spots)
    term = moves
    for m in range(3):
        term = term + gains[m] * places[m]
    term_hi = term.astype(BF16)
    term_lo = (term - term_hi.astype(F32)).astype(BF16)
    term_all = jnp.concatenate([term_hi[:, 0:HALF], term_hi[:, 0:HALF], term_lo[:, 0:HALF]], axis=1)
    moved = dot(term_all, above_all)

    n_cols = -(-n_vert * block // LANES) + 1
    columns = [None] * n_cols

    def put(q, value):
        columns[q] = value if columns[q] is None else columns[q] + value

    for i in range(n_vert):
        q, r = divmod(i * block, LANES)
        at = slice(i * LANES, (i + 1) * LANES)
        shaped = rows_of(tiles[i].astype(BF16).astype(F32))
        value = moved[:, at]
        for m in range(3):
            value = value + turns[m][:, at] * shaped[m]
        if r:
            value = pltpu.roll(value, r, 1)
        if r + block > LANES:
            put(q, jnp.where(lane8 >= r, value, 0.0))
            put(q + 1, jnp.where(lane8 < r, value, 0.0))
        else:
            put(q, value)
    width = n_vert * block
    for q in range(n_cols):
        size = min(LANES, width - q * LANES)
        if size > 0:
            value = columns[q].astype(out_ref.dtype)
            for a in range(3):
                out_ref[a, :, q * LANES : q * LANES + size] = value[own * a : own * (a + 1), 0:size]

    bas_copy.wait_send()

    @pl.when(first)
    def _():
        pass_copy.wait_send()

    @pl.when(jnp.logical_not(first))
    def _():
        each(0, n_src, lambda i: coeff_copy(i).wait_send())

    @pl.when(is_hub)
    def _():
        each(0, hub_index, lambda i: relay_copy(0, i).wait_send())
        each(hub_index + 1, n_src, lambda i: relay_copy(0, i).wait_send())
        each(0, n_src, lambda i: relay_copy(1, i).wait_send())

    @pl.when(group == groups - 1)
    def _():
        each(0, n_src, lambda i: skin_copy(i).wait_send())

    lead_copy.wait_send()
    each(1, n_src, lambda i: sent_copy(i).wait_send())


def body(n_vert, n_col, coeffs, shape_basis, template, regressor, quaternions, translation, parents, skin_index, skin_raw):
    own, total = coeffs.shape
    comps, _, block = shape_basis.shape
    joints = regressor.shape[0]
    slots = skin_index.shape[1]
    n_src = n_vert * (n_col // 2)
    anywhere = pl.BlockSpec(memory_space=pl.ANY)
    dma = pltpu.SemaphoreType.DMA
    out = pl.pallas_call(
        functools.partial(kernel, n_vert, n_col),
        out_shape=pltpu.VMEM((3, own, n_vert * block), BF16),
        in_specs=[anywhere] * 9,
        out_specs=pl.BlockSpec(memory_space=pltpu.VMEM),
        scratch_shapes=[
            pltpu.SMEM((joints,), jnp.int32),
            pltpu.VMEM((own, total), BF16),
            pltpu.VMEM((2, 3, block, comps), BF16),
            pltpu.VMEM((3, block), F32),
            pltpu.VMEM((joints, block), F32),
            pltpu.VMEM((own, 4, joints), F32),
            pltpu.VMEM((own, 3), F32),
            pltpu.VMEM((slots, block), jnp.int32),
            pltpu.VMEM((slots, block), F32),
            pltpu.VMEM((SUB, LANES), F32),
            pltpu.VMEM((n_col, own, LANES), BF16),
            pltpu.VMEM((n_src, 2, own, LANES), BF16),
            pltpu.VMEM((2, n_col, own, LANES), BF16),
            pltpu.VMEM((n_src * own, 2 * LANES), F32),
            pltpu.VMEM((2, slots, block), F32),
            pltpu.VMEM((n_vert, 2, slots, block), F32),
            pltpu.VMEM((3, LANES, block), F32),
            pltpu.VMEM((4 * LANES, 2 * LANES), F32),
            pltpu.VMEM((PARTS, 4 * LANES, 2 * LANES), BF16),
            pltpu.VMEM((4, LANES), F32),
            pltpu.VMEM((4, n_src * own, LANES), F32),
            pltpu.VMEM((SUB, LANES), F32),
            pltpu.VMEM((n_src * SUB, LANES), F32),
            pltpu.VMEM((n_src * SUB, LANES), F32),
            pltpu.VMEM((joints, SUB, LANES), F32),
            pltpu.VMEM((HALF * SUB, LANES), F32),
            pltpu.VMEM((HALF * SUB, LANES), F32),
            pltpu.VMEM((3, HALF * SUB, LANES), F32),
            pltpu.VMEM((HALF, n_vert * LANES), F32),
            dma((9,)),
            dma,
            dma,
            dma((n_src,)),
            dma((n_src,)),
            dma,
            dma((2,)),
            dma((2, n_src)),
            dma((n_src,)),
            dma((n_vert,)),
            dma((n_src,)),
            dma((n_src,)),
        ],
        compiler_params=pltpu.CompilerParams(collective_id=0, has_side_effects=True),
    )(
        parents,
        coeffs,
        jnp.transpose(shape_basis, (1, 2, 0)),
        template,
        regressor,
        quaternions,
        translation,
        jnp.transpose(skin_index),
        jnp.transpose(skin_raw),
    )
    return jnp.transpose(out, (1, 0, 2))


def solution(mesh):
    in_specs = (
        P(("vert", "col"), None),
        P("col", None, "vert"),
        P(None, "vert"),
        P(None, "vert"),
        P(("vert", "col"), None, None),
        P(("vert", "col"), None),
        P(),
        P("vert", None),
        P("vert", None),
    )
    out_specs = P(("vert", "col"), None, None)
    step = functools.partial(body, mesh.shape["vert"], mesh.shape["col"])
    return jax.shard_map(step, mesh=mesh, in_specs=in_specs, out_specs=out_specs, check_vma=False)
```

time: 16.5 us -> 15.8 us (0.958)
  Pallas kernels: 15.7 us -> 15.1 us
    pallas_call x1, Pallas kernels: 15.7 us -> 15.1 us  [body(): pl.pallas_call(functools.partial(kernel, n_vert, n_col), out_shape=pltpu....]
where the time goes in v2:
time: 15.8 us; the launch traced here: 15.7 us
  Pallas kernels  15.1 us (96%)
  local copies, waits for them, and re-layouts  0.6 us (4%)
    pallas_call x1, Pallas kernels, body(): pl.pallas_call(functools.partial(kernel, n_vert, n_col), out_shape=pltpu....  15.1 us
    unnamed x1, local copies, waits for them, and re-layouts  0.6 us

profile of v2, /device:TPU:0, one launch (start us, length us, event | category | flops | bytes accessed | tf_op | source)
XLA Modules:
  0.0 15.7 jit_solution(7186454067579798201)
XLA Ops:
  0.0 15.1 %shard_map.91 = bf16[3,2,656]{2,1,0:T(2,128)(2,1)S(1)} custom-call(s32[55]{0:T(128)} %parents_hbm.1, bf16[2,400]{1,0:T(2,128)(2,1)} %coeffs_hbm.1, bf16[3,82,100]{2,1,0:T(8,128)(2,1)} %bitcast.5, f32[3,82]{1,0:T(4,128)} %template_hbm.1, f32[55,82]{1,0:T(8,128)} %regressor_hbm.1, f32[2,4,55]{2,1,0:T(4,128)} %quat_hbm.1, f32[2,3]{1,0:T(2,128)} %shift_hbm.1, ...), custom_call_target="tpu_custom_call" | custom-call | tf_op jit(solution)/shard_map/pallas_call | solution.py:485
  15.1 0.6 %copy.11 = bf16[2,3,656]{2,0,1:T(2,128)(2,1)} copy(bf16[2,3,656]{2,0,1:T(2,128)(2,1)S(1)} %bitcast.4) | data formatting | bytes 15744

commit v3 on v2

--- a/solution.py
+++ b/solution.py
@@ -11,7 +11,7 @@
 LANES = 128
 HALF = 64
 SUB = 8
-PARTS = 3
+PARTS = 2
 F32 = jnp.float32
 BF16 = jnp.bfloat16
 EXACT = lax.Precision.HIGHEST
@@ -42,9 +42,9 @@
         lax.fori_loop(first, count, one, 0)
 
 
-def split(value):
+def split(value, count):
     parts = []
-    for _ in range(PARTS):
+    for _ in range(count):
         part = value.astype(BF16)
         value = value - part.astype(F32)
         parts.append(part)
@@ -98,6 +98,7 @@
     bas_r,
     coeff_s,
     coeff_r,
+    lead_r,
     passed_s,
     passed_r,
     relay_s,
@@ -152,7 +153,7 @@
     def _():
         hello((hub, 1))
 
-    each(1, n_src, lambda j: hello(across(n_src - j)))
+    each(1, n_src, lambda j: hello(across(j)))
 
     pairs = [
         (coeffs_hbm, coeff_in),
@@ -198,43 +199,39 @@
 
     bas_copy = remote(bas.at[side], bas.at[side], bas_s, bas_r, partner)
 
-    def bas_arrival():
-        remote(bas.at[1 - side], bas.at[1 - side], bas_s, bas_r, partner).wait_recv()
-
     def two(i):
         return pl.ds(2 * (i % groups), 2)
 
+    half = n_src // 2
+
+    def coeff_sem(i):
+        return coeff_r.at[i // half]
+
     def coeff_copy(i):
-        return remote(coeff_out.at[two(i)], coeff_got.at[mine], coeff_s.at[i], coeff_r.at[mine], across(i))
-
-    def coeff_arrival(i):
-        remote(coeff_out.at[pl.ds(0, 2)], coeff_got.at[i], coeff_s.at[i], coeff_r.at[i], across(i)).wait_recv()
+        return remote(coeff_out.at[two(i)], coeff_got.at[mine], coeff_s, coeff_sem(mine), across(i))
+
+    def arrival(ref, recv):
+        remote(ref, ref, bas_s, recv, partner).wait_recv()
+
+    def departure(ref, send):
+        remote(ref, ref, send, bas_r, partner).wait_send()
 
     pass_copy = remote(coeff_out, passed.at[side], passed_s, passed_r.at[side], (hub, 1))
 
-    def pass_arrival(k):
-        remote(coeff_out, passed.at[k], passed_s, passed_r.at[k], (0, k)).wait_recv()
-
     def relay_copy(k, i):
-        return remote(passed.at[k, two(i)], coeff_got.at[0], relay_s.at[k, i], coeff_r.at[0], place(i, 1 - k))
+        return remote(passed.at[k, two(i)], coeff_got.at[0], relay_s.at[k], lead_r, place(i, 1 - k))
 
     def skin_copy(i):
-        return remote(skin_out, skin_got.at[me], skin_s.at[i], skin_r.at[me], across(i))
-
-    def skin_arrival(v):
-        remote(skin_out, skin_got.at[v], skin_s.at[0], skin_r.at[v], partner).wait_recv()
+        return remote(skin_out, skin_got.at[me], skin_s.at[i // n_vert], skin_r, across(i))
 
     def tile(ref, i):
         start = i * SUB if isinstance(i, int) else pl.multiple_of(i * SUB, SUB)
         return ref.at[pl.ds(start, SUB)]
 
     def sent_copy(i):
-        return remote(tile(sent, i), tile(got, mine), sent_s.at[i], sent_r.at[mine], across(i))
-
-    lead_copy = remote(lead, tile(got, mine), sent_s.at[0], sent_r.at[mine], across(0))
-
-    def sent_arrival(i):
-        remote(tile(sent, i), tile(got, i), sent_s.at[i], sent_r.at[i], across(i)).wait_recv()
+        return remote(tile(sent.at[i // half], i % half), tile(got, mine), sent_s, sent_r, across(i))
+
+    lead_copy = remote(lead, tile(got, mine), sent_s, sent_r, across(0))
 
     hub_index = hub * groups
     expected = n_src + is_hub.astype(jnp.int32) * (n_src - 1)
@@ -245,22 +242,20 @@
     def _():
         pass_copy.start()
 
+    @pl.when(is_hub)
+    def _():
+        arrival(passed.at[0], passed_r.at[0])
+        each(0, half // 2, lambda j: relay_copy(0, n_src - 1 - j).start())
+        arrival(passed.at[1], passed_r.at[1])
+        each(0, half // 2, lambda j: relay_copy(1, n_src - 1 - j).start())
+        each(half // 2, n_src - 1 - hub_index, lambda j: relay_copy(0, n_src - 1 - j).start())
+        pltpu.make_async_copy(passed.at[0, two(hub_index)], coeff_got.at[0], lead_r).start()
+        each(half // 2, n_src, lambda j: relay_copy(1, n_src - 1 - j).start())
+        each(0, hub_index, lambda i: relay_copy(0, i).start())
+
     @pl.when(jnp.logical_not(first))
     def _():
         each(0, n_src, lambda j: coeff_copy(far_first(j)).start())
-
-    @pl.when(is_hub)
-    def _():
-        pass_arrival(0)
-        each(hub_index + 1, n_src, lambda i: relay_copy(0, i).start())
-        pltpu.make_async_copy(passed.at[0, two(hub_index)], coeff_got.at[0], coeff_r.at[0]).start()
-        each(0, hub_index, lambda i: relay_copy(0, i).start())
-        pass_arrival(1)
-        each(0, n_src, lambda j: relay_copy(1, n_src - 1 - j).start())
-
-    @pl.when(group == groups - 1)
-    def _():
-        each(0, n_src, lambda j: skin_copy(far_first(j)).start())
 
     for c in range(own):
         quat_rows[4 * c : 4 * c + 4, 0:joints] = quat[c]
@@ -299,17 +294,23 @@
     compose(0, (axis_lane == sub8).astype(F32))
     lax.fori_loop(1, joints, descend, 0)
 
+    @pl.when(group == groups - 1)
+    def _():
+        each(0, n_src, lambda j: skin_copy(far_first(j)).start())
+
     for m in range(3):
         spread[m, block:LANES, :] = regressor[0:room, :]
         spread[m, extra * m : extra * (m + 1), :] = regressor[room:joints, :]
     for m in range(3):
         base = dot_nt(template[...], spread[m], EXACT)[m : m + 1, :]
         spot = iota(base.shape, 1)
-        bias[m : m + 1, :] = jnp.where(spot >= block, base, 0.0)
-        bias[m : m + 1, 0:block] = template[m : m + 1, :]
+        at = m * LANES
+        bias[:, at : at + LANES] = jnp.where(spot >= block, base, 0.0)
+        bias[:, at : at + block] = template[m : m + 1, :]
         mark = (spot >= extra * m) & (spot < extra * (m + 1))
-        bias[3:4, :] = bias[3:4, :] + jnp.where(mark, base, 0.0)
-    spread_parts = [jnp.concatenate(split(spread[m]), axis=0) for m in range(3)]
+        bias[:, 3 * LANES :] = bias[:, 3 * LANES :] + jnp.where(mark, base, 0.0)
+    bias[...] = bias[...] * (group == 0).astype(F32)
+    spread_parts = [jnp.concatenate(split(spread[m], 3), axis=0) for m in range(3)]
 
     def lay(b, at):
         for m in range(3):
@@ -321,44 +322,75 @@
             row = 3 * LANES + extra * m
             wide[row : row + extra, at : at + comps] = sums[extra * m : extra * (m + 1)]
 
-    bas_arrival()
+    arrival(bas.at[1 - side], bas_r)
     for b in range(2):
         lay(b, b * LANES)
-    for p, part in enumerate(split(wide[...])):
-        table[p] = part
-
-    has_bias = (group == 0).astype(F32)
-
-    def partial(rows, q):
-        at = slice(q * LANES, (q + 1) * LANES)
-        value = bias[q : q + 1, :] * has_bias
-        for p in range(PARTS):
-            value = value + dot_nt(rows, table[p, at, :])
-        return value
-
-    coeff_arrival(0)
-    rows = jnp.concatenate([coeff_got[0, 0], coeff_got[0, 1]], axis=1)
-    lead[...] = jnp.concatenate([partial(rows, q) for q in range(4)], axis=0)
-    lead_copy.start()
-
-    each(1, n_src, coeff_arrival)
+    for p, part in enumerate(split(jnp.transpose(wide[...]), PARTS)):
+        table[p * 2 * LANES : (p + 1) * 2 * LANES, :] = part
+
+    def partial(rows):
+        return dot(jnp.concatenate([rows] * PARTS, axis=1), table[...]) + bias[...]
+
+    def lead_reply():
+        arrival(coeff_got.at[0], lead_r)
+        rows = jnp.concatenate([coeff_got[0, 0], coeff_got[0, 1]], axis=1)
+        value = partial(rows)
+        lead[...] = jnp.concatenate([value[:, q * LANES : (q + 1) * LANES] for q in range(4)], axis=0)
+        lead_copy.start()
+
     per = SUB // own
 
-    def gather(step):
-        for b in range(2):
-            rows = [coeff_got[step * per + i, b].astype(F32) for i in range(per)]
-            start = step * SUB if isinstance(step, int) else pl.multiple_of(step * SUB, SUB)
-            coeff_rows[pl.ds(start, SUB), b * LANES : (b + 1) * LANES] = jnp.concatenate(rows, axis=0)
-
-    each(0, n_src // per, gather)
-    rows = coeff_rows[...].astype(BF16)
-    for q in range(4):
-        product[q] = partial(rows, q)
-    for q in range(4):
-        for c in range(own):
-            value = product[q, pl.ds(c, n_src, stride=own), :]
-            sent[pl.ds(q * own + c, n_src, stride=SUB), :] = value
-    each(0, n_src - 1, lambda j: sent_copy(1 + j + (1 - upper) * (n_src - 2 - 2 * j)).start())
+    def batch(part):
+        start = part * half
+        skip = 1 - part
+        arrival(coeff_got.at[pl.ds(start + skip, half - skip)], coeff_r.at[part])
+
+        def source(i, b):
+            if isinstance(i, int) and i == 0 and part == 0:
+                return jnp.zeros((own, LANES), F32)
+            return coeff_got[start + i, b].astype(F32)
+
+        def gather(step):
+            at = step * SUB if isinstance(step, int) else pl.multiple_of(step * SUB, SUB)
+            for b in range(2):
+                rows = [source(step * per + i, b) for i in range(per)]
+                coeff_rows[pl.ds(at, SUB), b * LANES : (b + 1) * LANES] = jnp.concatenate(rows, axis=0)
+
+        gather(0)
+        each(1, half // per, gather)
+        rows = coeff_rows[...].astype(BF16)
+        value = partial(rows)
+        for q in range(4):
+            product[q] = value[:, q * LANES : (q + 1) * LANES]
+        for q in range(4):
+            for c in range(own):
+                sent[part, pl.ds(q * own + c, half, stride=SUB), :] = product[q, pl.ds(c, half, stride=own), :]
+
+        @pl.when((part == 1) & (upper == 0))
+        def _():
+            sent_copy(start + half - 1).start()
+
+        each(1, half, lambda j: sent_copy(start + far_in(j, part)).start())
+
+        @pl.when((part == 1) & (upper == 1))
+        def _():
+            sent_copy(start + half - 1).start()
+
+    def far_in(j, part):
+        ahead = j - part
+        behind = half - j - part
+        return ahead + (1 - upper) * (behind - ahead)
+
+    @pl.when(upper == 1)
+    def _():
+        lead_reply()
+
+    batch(1)
+    batch(0)
+
+    @pl.when(upper == 0)
+    def _():
+        lead_reply()
 
     def flipped(ref, m, n):
         value = ref[pl.ds(m, HALF, stride=SUB), :]
@@ -374,31 +406,60 @@
     moves = jnp.sum(jnp.where(iota(moves.shape, 1) == m_axis, moves, 0.0), axis=1, keepdims=True)
     moves = jnp.where(lane8 == joints, moves, 0.0)
 
-    each(0, n_vert, skin_arrival)
+    arrival(skin_got, skin_r)
     joint_row = iota((HALF, block), 0).astype(F32)
     for i in range(n_vert):
         grid = jnp.zeros((HALF, block), F32)
         for slot in range(slots):
             grid = jnp.where(skin_got[i, 0, slot : slot + 1, :] == joint_row, skin_got[i, 1, slot : slot + 1, :], grid)
-        weights[:, i * LANES : i * LANES + block] = grid
+        weights[:, i * block : (i + 1) * block] = grid
     blended = dot(factors, weights[...], EXACT)
     turns = [blended[m * SUB : (m + 1) * SUB] for m in range(3)]
     above_hi = blended[3 * SUB :].astype(BF16)
     above_lo = (blended[3 * SUB :] - above_hi.astype(F32)).astype(BF16)
     above_all = jnp.concatenate([above_hi, above_lo, above_hi], axis=0)
 
-    def rows_of(value):
+    packed = [jnp.where(lane8 >= block, pltpu.roll(gain, block, 1), 0.0) for gain in gains]
+    rest = jnp.zeros((SUB, LANES), F32)
+    for m in range(3):
+        mark = (lane8 >= extra * m) & (lane8 < extra * (m + 1))
+        rest = jnp.where(mark, pltpu.roll(gains[m], (extra * m - room) % LANES, 1), rest)
+    packed.append(rest)
+    moves = moves + pltpu.roll(moves, HALF, 1)
+
+    def rows_of(value, number):
         count = SUB // own
         spun = [value] + [pltpu.roll(value, own * q, 0) for q in range(1, count)]
         result = []
-        for m in range(3):
+        for m in range(number):
             one = spun[(-m) % count]
             for q in range(1, count):
                 one = jnp.where(sub8 // own == q, spun[(q - m) % count], one)
             result.append(one)
         return result
 
-    each(0, n_src, sent_arrival)
+    bas_copy.wait_send()
+
+    @pl.when(first)
+    def _():
+        pass_copy.wait_send()
+
+    @pl.when(jnp.logical_not(first))
+    def _():
+        departure(coeff_got, coeff_s)
+
+    @pl.when(is_hub)
+    def _():
+        departure(coeff_got.at[pl.ds(1, n_src - 1)], relay_s.at[0])
+        departure(coeff_got, relay_s.at[1])
+
+    @pl.when(group == groups - 1)
+    def _():
+        for q in range(groups):
+            departure(skin_got, skin_s.at[q])
+
+    departure(sent, sent_s)
+    arrival(got, sent_r)
     tiles = []
     for i in range(n_vert):
         at = i * groups * SUB
@@ -406,23 +467,27 @@
         for q in range(1, groups):
             value = value + got[at + q * SUB : at + (q + 1) * SUB, :]
         tiles.append(value)
-    summed = tiles[0]
-    for value in tiles[1:]:
-        summed = summed + value
-    spots = jnp.where(lane8 < room, pltpu.roll(summed, room, 1), 0.0)
-    for m in range(3):
-        moved = pltpu.roll(pltpu.roll(summed, (room - extra * m) % LANES, 1), (own * (m - 3)) % SUB, 0)
-        spots = jnp.where((sub8 // own == m) & (lane8 >= room) & (lane8 < joints), moved, spots)
-    places = rows_of(spots)
-    term = moves
-    for m in range(3):
-        term = term + gains[m] * places[m]
-    term_hi = term.astype(BF16)
-    term_lo = (term - term_hi.astype(F32)).astype(BF16)
-    term_all = jnp.concatenate([term_hi[:, 0:HALF], term_hi[:, 0:HALF], term_lo[:, 0:HALF]], axis=1)
-    moved = dot(term_all, above_all)
-
-    n_cols = -(-n_vert * block // LANES) + 1
+    summed = list(tiles)
+    while len(summed) > 1:
+        summed = [a + b for a, b in zip(summed[0::2], summed[1::2])] + summed[len(summed) // 2 * 2 :]
+    term = jnp.zeros((SUB, LANES), F32)
+    for gain, spots in zip(packed, rows_of(summed[0], 4)):
+        term = term + gain * spots
+    half_lane = lane8 % HALF
+    spread_out = moves
+    for at in (0, HALF):
+        near = pltpu.roll(term, (room + at) % LANES, 1)
+        far = jnp.zeros((SUB, LANES), F32)
+        for m in range(3):
+            far = far + pltpu.roll(term, (room + at - extra * m) % LANES, 1)
+        here = (lane8 >= at) & (lane8 < at + HALF)
+        spread_out = spread_out + jnp.where(here & (half_lane < room), near, 0.0)
+        spread_out = spread_out + jnp.where(here & (half_lane >= room) & (half_lane < joints), far, 0.0)
+    term_hi = spread_out.astype(BF16)
+    term_lo = (spread_out - term_hi.astype(F32)).astype(BF16)
+    moved = dot(jnp.concatenate([term_hi, term_lo[:, 0:HALF]], axis=1), above_all)
+
+    n_cols = -(-n_vert * block // LANES)
     columns = [None] * n_cols
 
     def put(q, value):
@@ -430,48 +495,22 @@
 
     for i in range(n_vert):
         q, r = divmod(i * block, LANES)
-        at = slice(i * LANES, (i + 1) * LANES)
-        shaped = rows_of(tiles[i].astype(BF16).astype(F32))
-        value = moved[:, at]
-        for m in range(3):
-            value = value + turns[m][:, at] * shaped[m]
+        value = tiles[i].astype(BF16).astype(F32)
         if r:
             value = pltpu.roll(value, r, 1)
+        put(q, jnp.where((lane8 >= r) & (lane8 < r + block), value, 0.0))
         if r + block > LANES:
-            put(q, jnp.where(lane8 >= r, value, 0.0))
-            put(q + 1, jnp.where(lane8 < r, value, 0.0))
-        else:
-            put(q, value)
+            put(q + 1, jnp.where(lane8 < r + block - LANES, value, 0.0))
     width = n_vert * block
     for q in range(n_cols):
+        at = slice(q * LANES, (q + 1) * LANES)
+        value = moved[:, at]
+        for m, shaped in enumerate(rows_of(columns[q], 3)):
+            value = value + turns[m][:, at] * shaped
+        value = value.astype(out_ref.dtype)
         size = min(LANES, width - q * LANES)
-        if size > 0:
-            value = columns[q].astype(out_ref.dtype)
-            for a in range(3):
-                out_ref[a, :, q * LANES : q * LANES + size] = value[own * a : own * (a + 1), 0:size]
-
-    bas_copy.wait_send()
-
-    @pl.when(first)
-    def _():
-        pass_copy.wait_send()
-
-    @pl.when(jnp.logical_not(first))
-    def _():
-        each(0, n_src, lambda i: coeff_copy(i).wait_send())
-
-    @pl.when(is_hub)
-    def _():
-        each(0, hub_index, lambda i: relay_copy(0, i).wait_send())
-        each(hub_index + 1, n_src, lambda i: relay_copy(0, i).wait_send())
-        each(0, n_src, lambda i: relay_copy(1, i).wait_send())
-
-    @pl.when(group == groups - 1)
-    def _():
-        each(0, n_src, lambda i: skin_copy(i).wait_send())
-
-    lead_copy.wait_send()
-    each(1, n_src, lambda i: sent_copy(i).wait_send())
+        for a in range(3):
+            out_ref[a, :, q * LANES : q * LANES + size] = value[own * a : own * (a + 1), 0:size]
 
 
 def body(n_vert, n_col, coeffs, shape_basis, template, regressor, quaternions, translation, parents, skin_index, skin_raw):
@@ -501,34 +540,35 @@
             pltpu.VMEM((n_col, own, LANES), BF16),
             pltpu.VMEM((n_src, 2, own, LANES), BF16),
             pltpu.VMEM((2, n_col, own, LANES), BF16),
-            pltpu.VMEM((n_src * own, 2 * LANES), F32),
+            pltpu.VMEM((n_src * own // 2, 2 * LANES), F32),
             pltpu.VMEM((2, slots, block), F32),
             pltpu.VMEM((n_vert, 2, slots, block), F32),
             pltpu.VMEM((3, LANES, block), F32),
             pltpu.VMEM((4 * LANES, 2 * LANES), F32),
-            pltpu.VMEM((PARTS, 4 * LANES, 2 * LANES), BF16),
-            pltpu.VMEM((4, LANES), F32),
-            pltpu.VMEM((4, n_src * own, LANES), F32),
+            pltpu.VMEM((PARTS * 2 * LANES, 4 * LANES), BF16),
+            pltpu.VMEM((1, 4 * LANES), F32),
+            pltpu.VMEM((4, n_src * own // 2, LANES), F32),
             pltpu.VMEM((SUB, LANES), F32),
-            pltpu.VMEM((n_src * SUB, LANES), F32),
+            pltpu.VMEM((2, n_src // 2 * SUB, LANES), F32),
             pltpu.VMEM((n_src * SUB, LANES), F32),
             pltpu.VMEM((joints, SUB, LANES), F32),
             pltpu.VMEM((HALF * SUB, LANES), F32),
             pltpu.VMEM((HALF * SUB, LANES), F32),
             pltpu.VMEM((3, HALF * SUB, LANES), F32),
-            pltpu.VMEM((HALF, n_vert * LANES), F32),
+            pltpu.VMEM((HALF, -(-n_vert * block // LANES) * LANES), F32),
             dma((9,)),
             dma,
             dma,
-            dma((n_src,)),
-            dma((n_src,)),
             dma,
             dma((2,)),
-            dma((2, n_src)),
-            dma((n_src,)),
-            dma((n_vert,)),
-            dma((n_src,)),
-            dma((n_src,)),
+            dma,
+            dma,
+            dma((2,)),
+            dma((2,)),
+            dma((n_col // 2,)),
+            dma,
+            dma,
+            dma,
         ],
         compiler_params=pltpu.CompilerParams(collective_id=0, has_side_effects=True),
     )(

time: 15.8 us -> 14.4 us (0.911)
  the two profiles are of different devices: /device:TPU:0 before, /device:TPU:1 now
where the time goes in v3:
time: 14.4 us; the launch traced here: 14.3 us
  Pallas kernels  13.7 us (95%)
  local copies, waits for them, and re-layouts  0.6 us (4%)
    pallas_call x1, Pallas kernels, body(): pl.pallas_call(functools.partial(kernel, n_vert, n_col), out_shape=pltpu....  13.7 us
    unnamed x1, local copies, waits for them, and re-layouts  0.6 us

profile of v3, /device:TPU:1, one launch (start us, length us, event | category | flops | bytes accessed | tf_op | source)
XLA Modules:
  0.0 14.3 jit_solution(8054416634097929252)
XLA Ops:
  0.0 13.7 %shard_map.91 = bf16[3,2,656]{2,1,0:T(2,128)(2,1)S(1)} custom-call(s32[55]{0:T(128)} %parents_hbm.1, bf16[2,400]{1,0:T(2,128)(2,1)} %coeffs_hbm.1, bf16[3,82,100]{2,1,0:T(8,128)(2,1)} %bitcast.5, f32[3,82]{1,0:T(4,128)} %template_hbm.1, f32[55,82]{1,0:T(8,128)} %regressor_hbm.1, f32[2,4,55]{2,1,0:T(4,128)} %quat_hbm.1, f32[2,3]{1,0:T(2,128)} %shift_hbm.1, ...), custom_call_target="tpu_custom_call" | custom-call | tf_op jit(solution)/shard_map/pallas_call | solution.py:524
  13.7 0.6 %copy.11 = bf16[2,3,656]{2,0,1:T(2,128)(2,1)} copy(bf16[2,3,656]{2,0,1:T(2,128)(2,1)S(1)} %bitcast.4) | data formatting | bytes 15744

commit v4 on v3

--- a/solution.py
+++ b/solution.py
@@ -76,6 +76,7 @@
     quat_rows,
     coeff_out,
     coeff_got,
+    lead_got,
     passed,
     coeff_rows,
     skin_out,
@@ -92,12 +93,15 @@
     state,
     diff,
     locals_ref,
+    factors,
     weights,
+    above,
     local_s,
     bas_s,
     bas_r,
     coeff_s,
     coeff_r,
+    lead_s,
     lead_r,
     passed_s,
     passed_r,
@@ -175,6 +179,7 @@
     axis_lane = jnp.minimum((lane8 % SUB) // own, 2)
     quat_rows[...] = jnp.zeros(quat_rows.shape, F32)
     weights[...] = jnp.zeros(weights.shape, F32)
+    factors[...] = jnp.zeros(factors.shape, F32)
     tree[...] = jnp.zeros(tree.shape, F32)
     state[...] = jnp.zeros(state.shape, F32)
     diff[...] = jnp.zeros(diff.shape, F32)
@@ -219,7 +224,7 @@
     pass_copy = remote(coeff_out, passed.at[side], passed_s, passed_r.at[side], (hub, 1))
 
     def relay_copy(k, i):
-        return remote(passed.at[k, two(i)], coeff_got.at[0], relay_s.at[k], lead_r, place(i, 1 - k))
+        return remote(passed.at[k, two(i)], lead_got.at[k], relay_s.at[k], lead_r.at[k], place(i, 1))
 
     def skin_copy(i):
         return remote(skin_out, skin_got.at[me], skin_s.at[i // n_vert], skin_r, across(i))
@@ -231,7 +236,8 @@
     def sent_copy(i):
         return remote(tile(sent.at[i // half], i % half), tile(got, mine), sent_s, sent_r, across(i))
 
-    lead_copy = remote(lead, tile(got, mine), sent_s, sent_r, across(0))
+    def lead_copy(k):
+        return remote(lead.at[k], tile(got, mine), sent_s if k == 0 else lead_s, sent_r, (0, k))
 
     hub_index = hub * groups
     expected = n_src + is_hub.astype(jnp.int32) * (n_src - 1)
@@ -248,10 +254,10 @@
         each(0, half // 2, lambda j: relay_copy(0, n_src - 1 - j).start())
         arrival(passed.at[1], passed_r.at[1])
         each(0, half // 2, lambda j: relay_copy(1, n_src - 1 - j).start())
-        each(half // 2, n_src - 1 - hub_index, lambda j: relay_copy(0, n_src - 1 - j).start())
-        pltpu.make_async_copy(passed.at[0, two(hub_index)], coeff_got.at[0], lead_r).start()
-        each(half // 2, n_src, lambda j: relay_copy(1, n_src - 1 - j).start())
-        each(0, hub_index, lambda i: relay_copy(0, i).start())
+        for k in range(2):
+            each(half // 2, n_src - 1 - hub_index, lambda j: relay_copy(k, n_src - 1 - j).start())
+            pltpu.make_async_copy(passed.at[k, two(hub_index)], lead_got.at[k], lead_r.at[k]).start()
+            each(0, hub_index, lambda i: relay_copy(k, i).start())
 
     @pl.when(jnp.logical_not(first))
     def _():
@@ -332,11 +338,24 @@
         return dot(jnp.concatenate([rows] * PARTS, axis=1), table[...]) + bias[...]
 
     def lead_reply():
-        arrival(coeff_got.at[0], lead_r)
-        rows = jnp.concatenate([coeff_got[0, 0], coeff_got[0, 1]], axis=1)
-        value = partial(rows)
-        lead[...] = jnp.concatenate([value[:, q * LANES : (q + 1) * LANES] for q in range(4)], axis=0)
-        lead_copy.start()
+        rows = []
+        for k in range(2):
+            arrival(lead_got.at[k], lead_r.at[k])
+        for k in range(2):
+            rows.append(jnp.concatenate([lead_got[k, 0], lead_got[k, 1]], axis=1).astype(F32))
+        value = partial(jnp.concatenate(rows, axis=0).astype(BF16))
+        for k in range(2):
+            part = value[own * k : own * (k + 1)]
+            lead[k] = jnp.concatenate([part[:, q * LANES : (q + 1) * LANES] for q in range(4)], axis=0)
+        lead_copy(0).start()
+
+        @pl.when(mine > 0)
+        def _():
+            lead_copy(1).start()
+
+        @pl.when(mine == 0)
+        def _():
+            pltpu.make_async_copy(lead.at[1], tile(got, mine), sent_r).start()
 
     per = SUB // own
 
@@ -381,14 +400,14 @@
         behind = half - j - part
         return ahead + (1 - upper) * (behind - ahead)
 
-    @pl.when(upper == 1)
+    @pl.when((upper == 1) & (side == 1))
     def _():
         lead_reply()
 
     batch(1)
     batch(0)
 
-    @pl.when(upper == 0)
+    @pl.when((upper == 0) & (side == 1))
     def _():
         lead_reply()
 
@@ -398,13 +417,18 @@
 
     gains = [flipped(diff, m, SUB) for m in range(3)]
     gains = [jnp.where(lane8 < HALF, gain, 0.0) for gain in gains]
-    factors = jnp.concatenate(
-        [flipped(state, m, SUB)[:, 0:HALF] for m in range(3)] + [flipped(state, 3, HALF)[:, 0:HALF]], axis=0
-    )
+    for m in range(3):
+        factors[m * SUB : (m + 1) * SUB, :] = flipped(state, m, SUB)[:, 0:HALF]
+    line = flipped(state, 3, HALF)[:, 0:HALF]
+    factors[3 * SUB + block : 3 * SUB + LANES, :] = line[0:room]
+    for m in range(3):
+        factors[3 * SUB + extra * m : 3 * SUB + extra * (m + 1), :] = line[room:joints]
+    spare = 3 * extra
+    factors[3 * SUB + spare : 3 * SUB + spare + 1, :] = line[joints : joints + 1]
     moves = jnp.concatenate([shift[...]] * (SUB // own), axis=0)
     m_axis = jnp.minimum(iota(moves.shape, 0) // own, 2)
     moves = jnp.sum(jnp.where(iota(moves.shape, 1) == m_axis, moves, 0.0), axis=1, keepdims=True)
-    moves = jnp.where(lane8 == joints, moves, 0.0)
+    moves = jnp.where(lane8 == spare, moves, 0.0)
 
     arrival(skin_got, skin_r)
     joint_row = iota((HALF, block), 0).astype(F32)
@@ -413,11 +437,13 @@
         for slot in range(slots):
             grid = jnp.where(skin_got[i, 0, slot : slot + 1, :] == joint_row, skin_got[i, 1, slot : slot + 1, :], grid)
         weights[:, i * block : (i + 1) * block] = grid
-    blended = dot(factors, weights[...], EXACT)
+    blended = dot(factors[...], weights[...], EXACT)
     turns = [blended[m * SUB : (m + 1) * SUB] for m in range(3)]
     above_hi = blended[3 * SUB :].astype(BF16)
     above_lo = (blended[3 * SUB :] - above_hi.astype(F32)).astype(BF16)
-    above_all = jnp.concatenate([above_hi, above_lo, above_hi], axis=0)
+    above[0:LANES, :] = above_hi
+    above[LANES : 2 * LANES, :] = above_hi
+    above[2 * LANES :, :] = above_lo
 
     packed = [jnp.where(lane8 >= block, pltpu.roll(gain, block, 1), 0.0) for gain in gains]
     rest = jnp.zeros((SUB, LANES), F32)
@@ -425,7 +451,6 @@
         mark = (lane8 >= extra * m) & (lane8 < extra * (m + 1))
         rest = jnp.where(mark, pltpu.roll(gains[m], (extra * m - room) % LANES, 1), rest)
     packed.append(rest)
-    moves = moves + pltpu.roll(moves, HALF, 1)
 
     def rows_of(value, number):
         count = SUB // own
@@ -450,15 +475,25 @@
 
     @pl.when(is_hub)
     def _():
-        departure(coeff_got.at[pl.ds(1, n_src - 1)], relay_s.at[0])
-        departure(coeff_got, relay_s.at[1])
+        for k in range(2):
+            departure(coeff_got.at[pl.ds(1, n_src - 1)], relay_s.at[k])
 
     @pl.when(group == groups - 1)
     def _():
         for q in range(groups):
             departure(skin_got, skin_s.at[q])
 
-    departure(sent, sent_s)
+    @pl.when(side == 1)
+    def _():
+        departure(got, sent_s)
+
+    @pl.when(side == 0)
+    def _():
+        departure(got.at[pl.ds(SUB, (n_src - 1) * SUB)], sent_s)
+
+    @pl.when((side == 1) & (mine > 0))
+    def _():
+        departure(lead.at[1], lead_s)
     arrival(got, sent_r)
     tiles = []
     for i in range(n_vert):
@@ -470,22 +505,12 @@
     summed = list(tiles)
     while len(summed) > 1:
         summed = [a + b for a, b in zip(summed[0::2], summed[1::2])] + summed[len(summed) // 2 * 2 :]
-    term = jnp.zeros((SUB, LANES), F32)
+    term = moves
     for gain, spots in zip(packed, rows_of(summed[0], 4)):
         term = term + gain * spots
-    half_lane = lane8 % HALF
-    spread_out = moves
-    for at in (0, HALF):
-        near = pltpu.roll(term, (room + at) % LANES, 1)
-        far = jnp.zeros((SUB, LANES), F32)
-        for m in range(3):
-            far = far + pltpu.roll(term, (room + at - extra * m) % LANES, 1)
-        here = (lane8 >= at) & (lane8 < at + HALF)
-        spread_out = spread_out + jnp.where(here & (half_lane < room), near, 0.0)
-        spread_out = spread_out + jnp.where(here & (half_lane >= room) & (half_lane < joints), far, 0.0)
-    term_hi = spread_out.astype(BF16)
-    term_lo = (spread_out - term_hi.astype(F32)).astype(BF16)
-    moved = dot(jnp.concatenate([term_hi, term_lo[:, 0:HALF]], axis=1), above_all)
+    term_hi = term.astype(BF16)
+    term_lo = (term - term_hi.astype(F32)).astype(BF16)
+    moved = dot(jnp.concatenate([term_hi, term_lo], axis=1), above[0 : 2 * LANES, :]) + dot(term_hi, above[2 * LANES :, :])
 
     n_cols = -(-n_vert * block // LANES)
     columns = [None] * n_cols
@@ -539,6 +564,7 @@
             pltpu.VMEM((SUB, LANES), F32),
             pltpu.VMEM((n_col, own, LANES), BF16),
             pltpu.VMEM((n_src, 2, own, LANES), BF16),
+            pltpu.VMEM((2, 2, own, LANES), BF16),
             pltpu.VMEM((2, n_col, own, LANES), BF16),
             pltpu.VMEM((n_src * own // 2, 2 * LANES), F32),
             pltpu.VMEM((2, slots, block), F32),
@@ -548,20 +574,23 @@
             pltpu.VMEM((PARTS * 2 * LANES, 4 * LANES), BF16),
             pltpu.VMEM((1, 4 * LANES), F32),
             pltpu.VMEM((4, n_src * own // 2, LANES), F32),
-            pltpu.VMEM((SUB, LANES), F32),
+            pltpu.VMEM((2, SUB, LANES), F32),
             pltpu.VMEM((2, n_src // 2 * SUB, LANES), F32),
             pltpu.VMEM((n_src * SUB, LANES), F32),
             pltpu.VMEM((joints, SUB, LANES), F32),
             pltpu.VMEM((HALF * SUB, LANES), F32),
             pltpu.VMEM((HALF * SUB, LANES), F32),
             pltpu.VMEM((3, HALF * SUB, LANES), F32),
+            pltpu.VMEM((3 * SUB + LANES, HALF), F32),
             pltpu.VMEM((HALF, -(-n_vert * block // LANES) * LANES), F32),
+            pltpu.VMEM((3 * LANES, -(-n_vert * block // LANES) * LANES), BF16),
             dma((9,)),
             dma,
             dma,
             dma,
             dma((2,)),
             dma,
+            dma((2,)),
             dma,
             dma((2,)),
             dma((2,)),

time: 14.4 us -> 14.2 us (0.986)
  the two profiles are of different devices: /device:TPU:1 before, /device:TPU:0 now
where the time goes in v4:
time: 14.2 us; the launch traced here: 14.1 us
  Pallas kernels  13.5 us (95%)
  local copies, waits for them, and re-layouts  0.6 us (4%)
    pallas_call x1, Pallas kernels, body(): pl.pallas_call(functools.partial(kernel, n_vert, n_col), out_shape=pltpu....  13.5 us
    unnamed x1, local copies, waits for them, and re-layouts  0.6 us

profile of v4, /device:TPU:0, one launch (start us, length us, event | category | flops | bytes accessed | tf_op | source)
XLA Modules:
  0.0 14.1 jit_solution(15862130444819321152)
XLA Ops:
  0.0 13.5 %shard_map.91 = bf16[3,2,656]{2,1,0:T(2,128)(2,1)S(1)} custom-call(s32[55]{0:T(128)} %parents_hbm.1, bf16[2,400]{1,0:T(2,128)(2,1)} %coeffs_hbm.1, bf16[3,82,100]{2,1,0:T(8,128)(2,1)} %bitcast.5, f32[3,82]{1,0:T(4,128)} %template_hbm.1, f32[55,82]{1,0:T(8,128)} %regressor_hbm.1, f32[2,4,55]{2,1,0:T(4,128)} %quat_hbm.1, f32[2,3]{1,0:T(2,128)} %shift_hbm.1, ...), custom_call_target="tpu_custom_call" | custom-call | tf_op jit(solution)/shard_map/pallas_call | solution.py:549
  13.5 0.6 %copy.11 = bf16[2,3,656]{2,0,1:T(2,128)(2,1)} copy(bf16[2,3,656]{2,0,1:T(2,128)(2,1)S(1)} %bitcast.4) | data formatting | bytes 15744
